TPU v7x, 32 devices: a whole 2x2x4 slice. The times are simulated.
32 devices in a mesh: grp: 16 (over z, x, core), fsdp: 2 (over y).
Axes of the slice: x: 2, y: 2, z: 4, core: 2. Of those that a mesh axis runs over, the one named last changes fastest.
Arguments:
- tokens: bfloat16 [12288, 3584], P(('grp', 'fsdp')), may hold values from -6 to 6
- target: bfloat16 [12288, 1024], P(('grp', 'fsdp')), may hold values from -6 to 6
- weight: bfloat16 [3584, 1024], P('fsdp'), may hold values from -0.09375 to 0.09375
- factor_a: bfloat16 [3584, 512], P('fsdp'), may hold values from -6 to 6
- factor_b: bfloat16 [512, 1024], replicated, may hold values from -6 to 6
- counts: int32 [256], replicated, may hold values from 1 to 192, 12288 in all
- cand_index: int32 [256, 2], replicated, may hold values from 0 to 511
Outputs:
- update: float32 [3584, 1024], P('fsdp')
- scores: float32 [256], replicated
Inputs may be any that keep to these rules, and one draw needn't show every extreme that they name: The counts sum to 12288; candidate i owns the tokens from counts[0] + ... + counts[i-1] on.
All inputs are finite; a program needn't handle non-finite values.
Results may differ from a plain program's by a relative error of at most 0.003.
Values may be sent and summed in bfloat16 or wider, within the bound.
No kernel may reach another device: no remote copies, remote signals or barrier semaphores. Data moves between devices by JAX's collectives and lax.ppermute only.
A program may use at most 64 MiB of HBM per device.

v0:
```python
import jax
import jax.numpy as jnp
from jax import lax
from jax.sharding import PartitionSpec as P

D = 3584


def per_device(tokens, target, weight, factor_a, factor_b, counts, cand_index):
    rows = tokens.shape[0]
    width_out = weight.shape[1]
    pool_size = factor_a.shape[1]
    total_cands = counts.shape[0]
    noise = 0.5 * D ** (-0.5)
    spread_rows = lax.all_to_all(tokens, "fsdp", split_axis=1, concat_axis=0, tiled=True)
    joined = jnp.concatenate((weight, factor_a), axis=1)
    summed = lax.psum_scatter(
        jnp.dot(spread_rows, joined, preferred_element_type=jnp.float32),
        "fsdp",
        scatter_dimension=0,
        tiled=True,
    )
    base = summed[:, :width_out]
    pool_scores = summed[:, width_out:]
    ends = jnp.cumsum(counts)
    position = lax.axis_index(("grp", "fsdp")) * rows + jnp.arange(rows, dtype=jnp.int32)
    owner = jnp.sum((ends[None, :] <= position[:, None]).astype(jnp.int32), axis=1)
    left_index = cand_index[:, 0]
    right_index = cand_index[:, 1]
    tok_a = jnp.take(left_index, owner)
    tok_b = jnp.take(right_index, owner)
    pool_ids = jnp.arange(pool_size, dtype=jnp.int32)
    picked = jnp.sum(jnp.where(tok_a[:, None] == pool_ids[None, :], pool_scores, 0.0), axis=1)
    right_rows = jnp.take(factor_b, tok_b, axis=0).astype(jnp.float32)
    output = base + noise * picked[:, None] * right_rows
    diff = output - target.astype(jnp.float32)
    loss = jnp.mean(diff * diff, axis=1)
    cand_ids = jnp.arange(total_cands, dtype=jnp.int32)
    partial_value = jnp.sum(
        jnp.where(owner[:, None] == cand_ids[None, :], loss[:, None], 0.0), axis=0
    )
    totals = lax.psum(partial_value, ("grp", "fsdp"))
    fitness = -totals / counts.astype(jnp.float32)
    middle = jnp.mean(fitness)
    variance = jnp.mean((fitness - middle) ** 2)
    scores = (fitness - middle) / jnp.sqrt(variance + 1e-06)
    selector = (pool_ids[:, None] == left_index[None, :]).astype(jnp.bfloat16)
    columns = jnp.dot(factor_a, selector, preferred_element_type=jnp.float32)
    scaled = (columns * scores[None, :]).astype(jnp.bfloat16)
    chosen_rows = jnp.take(factor_b, right_index, axis=0)
    summed_update = jnp.dot(scaled, chosen_rows, preferred_element_type=jnp.float32)
    update = summed_update / jnp.sqrt(jnp.float32(total_cands))
    return (update, scores)


def solution(mesh):
    in_specs = (
        P(("grp", "fsdp"), None),
        P(("grp", "fsdp"), None),
        P("fsdp", None),
        P("fsdp", None),
        P(),
        P(),
        P(),
    )
    out_specs = (P("fsdp", None), P())
    return jax.shard_map(
        per_device, mesh=mesh, in_specs=in_specs, out_specs=out_specs, check_vma=False
    )
```

profile of v0, /device:TPU:0, one launch (start us, length us, event | category | flops | bytes accessed | tf_op | source)
XLA Modules:
  0.0 185.1 jit_solution(5749809767784370416)
XLA Ops:
  7.2 0.0 copy-start
  7.2 0.0 reduce-scatter.2.cloned.1.call-start
  7.2 4.6 %copy.17 = bf16[384,3584]{0,1:T(8,128)(2,1)} copy(bf16[384,3584]{1,0:T(8,128)(2,1)} %param.9) | data formatting | bytes 5505024 | tf_op args[0]
  11.8 39.5 %all_to_all.19 = bf16[384,2,1792]{0,2,1:T(8,128)(2,1)} all-to-all(bf16[384,2,1792]{0,2,1:T(8,128)(2,1)} %bitcast.17), channel_id=1, replica_groups=mesh['grp'=16,'fsdp'=2] {'fsdp'}, dimensions={1} | all-to-all | bytes 5505024 | tf_op jit(solution)/shard_map/all_to_all | solution.py:15
  51.3 0.0 copy-start.1
  51.3 4.8 %copy.18 = bf16[2,384,1792]{2,1,0:T(8,128)(2,1)} copy(bf16[2,384,1792]{1,2,0:T(8,128)(2,1)} %bitcast.16) | data formatting | bytes 5505024 | tf_op jit(solution)/shard_map/all_to_all | solution.py:15
  56.1 0.0 copy-done.1
  56.1 9.6 %fusion.4 = f32[768,1536]{0,1:T(8,128)} fusion(bf16[768,1792]{1,0:T(8,128)(2,1)} %bitcast.18, bf16[1792,512]{1,0:T(8,128)(2,1)S(1)} %copy-done.1, bf16[1792,1024]{1,0:T(8,128)(2,1)} %param.11), kind=kOutput, calls=%fused_computation.9 | convolution fusion | flops 4238868480 | bytes 12976128 | tf_op jit(solution)/shard_map/dot_general | solution.py:18
  65.7 0.0 copy-start.4
  65.7 0.0 copy-start.3
  65.7 0.0 reduce-scatter.2.cloned.1.call-update
  65.7 0.6 copy-done.4
  66.4 0.3 reduce-window.9
  66.7 0.1 slice.20
  66.8 0.1 slice_reduce_fusion
  66.9 0.1 add_bitcast_fusion
  67.0 0.2 convert_reduce_fusion
  67.3 0.0 copy-done.3
  67.3 2.8 %gather_fusion.2 = s32[384]{0:T(512)S(1)} fusion(s32[256]{0:T(256)S(1)} %bitcast.13, s32[1024]{0:T(1024)S(1)} %pad_clamp_fusion.2), kind=kCustom, calls=%fused_computation.clone | custom fusion | bytes 4608 | tf_op jit(solution)/shard_map/jit(_take)/gather | solution.py:30
  70.1 2.8 %gather_fusion.3 = s32[384]{0:T(512)S(1)} fusion(s32[256]{0:T(256)S(1)} %bitcast.15, s32[1024]{0:T(1024)S(1)} %pad_clamp_fusion.2), kind=kCustom, calls=%fused_computation.1.clone | custom fusion | bytes 4608 | tf_op jit(solution)/shard_map/jit(_take)/gather | solution.py:31
  72.9 0.0 copy-done
  72.9 0.0 copy-start.2
  73.0 2.1 %gather_fusion = bf16[384,1024]{1,0:T(8,128)(2,1)S(1)} fusion(bf16[512,1024]{1,0:T(8,128)(2,1)S(1)} %copy-done, s32[1024]{0:T(1024)S(1)} %pad_clamp_fusion.1), kind=kCustom, calls=%fused_computation.2 | custom fusion | bytes 1574400 | tf_op jit(solution)/shard_map/jit(_take)/gather | solution.py:34
  75.0 0.4 copy.19
  75.4 0.0 copy-done.2
  75.4 0.4 copy.20
  75.8 1.2 gather_fusion.1
  77.0 49.5 %reduce-scatter.2.cloned.1.call-done = f32[384,1536]{0,1:T(8,128)} async-done(((f32[768,1536]{0,1:T(8,128)}), f32[384,1536]{0,1:T(8,128)}) %reduce-scatter.2.cloned.1.call-update) | async-done | bytes 2359312 | tf_op jit(solution)/shard_map/reduce_scatter | solution.py:17
  126.5 1.3 fusion.12
  127.7 1.9 fusion.10
  129.6 0.2 select_reduce_fusion
  129.8 39.5 %psum.7 = f32[256]{0:T(256)S(1)} all-reduce(f32[256]{0:T(256)S(1)} %select_reduce_fusion), channel_id=1, replica_groups=mesh['grp'=16,'fsdp'=2] {'grp','fsdp'}, use_global_device_ids=true, to_apply=%region_7.9 | all-reduce | flops 256 | bytes 2048 | tf_op jit(solution)/shard_map/psum | solution.py:42
  169.3 0.6 fusion.23
  170.5 0.6 multiply_reduce_fusion
  171.8 0.0 copy-start.5
  171.9 6.4 %convolution_multiply_fusion = f32[1792,1024]{1,0:T(8,128)} fusion(bf16[1792,512]{1,0:T(8,128)(2,1)} %param.12, f32[256]{0:T(256)S(1)} %subtract_divide_fusion, bf16[256,1024]{1,0:T(8,128)(2,1)S(1)} %gather_fusion.1, pred[256]{0:T(512)(128)(4,1)S(1)} %get-tuple-element.3, s32[256]{0:T(256)S(1)} %bitcast.14), kind=kOutput, calls=%fused_computation.8 | convolution fusion | flops 1412562944 | bytes 9701632 | tf_op jit(solution)/shard_map/dot_general | solution.py:51
  178.3 0.0 copy-done.5
  (13 shorter events, 0.1 us)
Async XLA Ops:
  7.2 65.8 %copy-start = (bf16[512,1024]{1,0:T(8,128)(2,1)S(1)}, bf16[512,1024]{1,0:T(8,128)(2,1)}, u32[]{:S(2)}) copy-start(bf16[512,1024]{1,0:T(8,128)(2,1)} %param.13) | copy-start | bytes 3145732
  7.2 119.3 %reduce-scatter.2.cloned.1.call-start = ((), (), s32[]{:S(2)}) async-start(), calls=%async_computation.2 | async-start | bytes 7077888 | tf_op jit(solution)/shard_map/reduce_scatter | solution.py:17
  51.3 4.8 %copy-start.1 = (bf16[1792,512]{1,0:T(8,128)(2,1)S(1)}, bf16[1792,512]{1,0:T(8,128)(2,1)}, u32[]{:S(2)}) copy-start(bf16[1792,512]{1,0:T(8,128)(2,1)} %param.12) | copy-start | bytes 5505028
  65.7 0.7 copy-start.4
  65.7 1.5 copy-start.3
  72.9 2.5 %copy-start.2 = (bf16[384,1024]{1,0:T(8,128)(2,1)S(1)}, bf16[384,1024]{1,0:T(8,128)(2,1)}, u32[]{:S(2)}) copy-start(bf16[384,1024]{1,0:T(8,128)(2,1)} %param.10) | copy-start | bytes 2359300
  171.8 6.4 %copy-start.5 = (f32[256]{0:T(256)}, f32[256]{0:T(256)S(1)}, u32[]{:S(2)}) copy-start(f32[256]{0:T(256)S(1)} %subtract_divide_fusion) | copy-start | bytes 3076
Sparse Core Ops, SparseCore 0:
  65.9 60.5 reduce-scatter.1
where the time goes:
time: 186 us; the launch traced here: 185 us
  blocking collectives  79 us (42%)
  waiting for transfers between devices  49.5 us (27%)
  local copies, waits for them, and re-layouts  19.8 us (11%)
  matrix products  16 us (9%)
  between operations  15.5 us (8%)
  other arithmetic  5.24 us (3%)
    reduce_scatter x1, waiting for transfers between devices, per_device(): lax.psum_scatter(jnp.dot(spread_rows, joined, preferred_element_type=jnp....  49.5 us
    all_to_all x1, blocking collectives, per_device(): lax.all_to_all(tokens, 'fsdp', split_axis=1, concat_axis=0, tiled=True)  39.5 us
    psum x1, blocking collectives, per_device(): totals = lax.psum(partial_value, ('grp', 'fsdp'))  39.5 us
    dot_general x1, matrix products, per_device(): jnp.dot(spread_rows, joined, preferred_element_type=jnp.float32)  9.63 us
    dot_general x1, matrix products, per_device(): jnp.dot(scaled, chosen_rows, preferred_element_type=jnp.float32)  6.42 us
    unnamed x14, local copies, waits for them, and re-layouts  5.6 us
    all_to_all x1, local copies, waits for them, and re-layouts, per_device(): lax.all_to_all(tokens, 'fsdp', split_axis=1, concat_axis=0, tiled=True)  4.77 us
  transfers between devices with their start and end apart: 1, of which 1 were waited for; matrix products, arithmetic and copies ran while one was open for 6% of the time, Pallas kernels for 0%

commit v1 on v0

--- a/solution.py
+++ b/solution.py
@@ -39,7 +39,7 @@
     partial_value = jnp.sum(
         jnp.where(owner[:, None] == cand_ids[None, :], loss[:, None], 0.0), axis=0
     )
-    totals = lax.psum(partial_value, ("grp", "fsdp"))
+    totals = jnp.sum(jax.lax.all_gather(partial_value, ("grp", "fsdp")), 0)
     fitness = -totals / counts.astype(jnp.float32)
     middle = jnp.mean(fitness)
     variance = jnp.mean((fitness - middle) ** 2)

time: 186 us -> 213 us (1.15)
  blocking collectives: 79 us -> 106 us
    all_gather x0 -> x1, blocking collectives: none -> 66.9 us  [per_device(): totals = jnp.sum(jax.lax.all_gather(partial_value, ('grp', 'fsdp')), 0)]
    psum x1 -> x0, blocking collectives: 39.5 us -> none  [per_device(): totals = lax.psum(partial_value, ('grp', 'fsdp'))]
  transfers between devices with their start and end apart: 1 -> 1, of which waited for: 1 -> 1; matrix products, arithmetic and copies ran while one was open for 6% -> 5% of each run, Pallas kernels for 0% -> 0%
where the time goes in v1:
time: 213 us
  blocking collectives  106 us (50%)
  waiting for transfers between devices  49.5 us (23%)
  local copies, waits for them, and re-layouts  19.8 us (9%)
  matrix products  16.1 us (8%)
  between operations  15.5 us (7%)
  other arithmetic  5.3 us (2%)
    all_gather x1, blocking collectives, per_device(): totals = jnp.sum(jax.lax.all_gather(partial_value, ('grp', 'fsdp')), 0)  66.9 us
    reduce_scatter x1, waiting for transfers between devices, per_device(): lax.psum_scatter(jnp.dot(spread_rows, joined, preferred_element_type=jnp....  49.5 us
    all_to_all x1, blocking collectives, per_device(): lax.all_to_all(tokens, 'fsdp', split_axis=1, concat_axis=0, tiled=True)  39.5 us
    dot_general x1, matrix products, per_device(): jnp.dot(spread_rows, joined, preferred_element_type=jnp.float32)  9.63 us
    dot_general x1, matrix products, per_device(): jnp.dot(scaled, chosen_rows, preferred_element_type=jnp.float32)  6.43 us
    unnamed x14, local copies, waits for them, and re-layouts  5.6 us
    all_to_all x1, local copies, waits for them, and re-layouts, per_device(): lax.all_to_all(tokens, 'fsdp', split_axis=1, concat_axis=0, tiled=True)  4.77 us
  transfers between devices with their start and end apart: 1, of which 1 were waited for; matrix products, arithmetic and copies ran while one was open for 5% of the time, Pallas kernels for 0%

profile of v1, /device:TPU:0, one launch (start us, length us, event | category | flops | bytes accessed | tf_op | source)
XLA Modules:
  0.0 212.6 jit_solution(4402080190296923553)
XLA Ops:
  7.2 0.0 copy-start
  7.2 0.0 reduce-scatter.2.cloned.1.call-start
  7.2 4.6 %copy.21 = bf16[384,3584]{0,1:T(8,128)(2,1)} copy(bf16[384,3584]{1,0:T(8,128)(2,1)} %param.9) | data formatting | bytes 5505024 | tf_op args[0]
  11.8 39.5 %all_to_all.19 = bf16[384,2,1792]{0,2,1:T(8,128)(2,1)} all-to-all(bf16[384,2,1792]{0,2,1:T(8,128)(2,1)} %bitcast.18), channel_id=1, replica_groups=mesh['grp'=16,'fsdp'=2] {'fsdp'}, dimensions={1} | all-to-all | bytes 5505024 | tf_op jit(solution)/shard_map/all_to_all | solution.py:15
  51.3 0.0 copy-start.1
  51.3 4.8 %copy.22 = bf16[2,384,1792]{2,1,0:T(8,128)(2,1)} copy(bf16[2,384,1792]{1,2,0:T(8,128)(2,1)} %bitcast.17) | data formatting | bytes 5505024 | tf_op jit(solution)/shard_map/all_to_all | solution.py:15
  56.1 0.0 copy-done.1
  56.1 9.6 %fusion.4 = f32[768,1536]{0,1:T(8,128)} fusion(bf16[768,1792]{1,0:T(8,128)(2,1)} %bitcast.19, bf16[1792,512]{1,0:T(8,128)(2,1)S(1)} %copy-done.1, bf16[1792,1024]{1,0:T(8,128)(2,1)} %param.11), kind=kOutput, calls=%fused_computation.9 | convolution fusion | flops 4238868480 | bytes 12976128 | tf_op jit(solution)/shard_map/dot_general | solution.py:18
  65.7 0.0 copy-start.4
  65.7 0.0 copy-start.3
  65.7 0.0 reduce-scatter.2.cloned.1.call-update
  65.8 0.6 copy-done.4
  66.4 0.3 reduce-window.9
  66.7 0.1 slice.20
  66.8 0.1 slice_reduce_fusion
  66.9 0.1 add_bitcast_fusion
  67.0 0.2 convert_reduce_fusion
  67.3 0.0 copy-done.3
  67.3 2.8 %gather_fusion.2 = s32[384]{0:T(512)S(1)} fusion(s32[256]{0:T(256)S(1)} %bitcast.14, s32[1024]{0:T(1024)S(1)} %pad_clamp_fusion.2), kind=kCustom, calls=%fused_computation.clone | custom fusion | bytes 4608 | tf_op jit(solution)/shard_map/jit(_take)/gather | solution.py:30
  70.1 2.8 %gather_fusion.3 = s32[384]{0:T(512)S(1)} fusion(s32[256]{0:T(256)S(1)} %bitcast.16, s32[1024]{0:T(1024)S(1)} %pad_clamp_fusion.2), kind=kCustom, calls=%fused_computation.1.clone | custom fusion | bytes 4608 | tf_op jit(solution)/shard_map/jit(_take)/gather | solution.py:31
  72.9 0.0 copy-done
  73.0 0.0 copy-start.2
  73.0 2.1 gather_fusion
  75.0 0.4 copy.23
  75.4 0.0 copy-done.2
  75.4 0.4 copy.24
  75.8 1.2 gather_fusion.1
  77.0 49.5 %reduce-scatter.2.cloned.1.call-done = f32[384,1536]{0,1:T(8,128)} async-done(((f32[768,1536]{0,1:T(8,128)}), f32[384,1536]{0,1:T(8,128)}) %reduce-scatter.2.cloned.1.call-update) | async-done | bytes 2359312 | tf_op jit(solution)/shard_map/reduce_scatter | solution.py:17
  126.5 1.3 fusion.12
  127.7 1.9 fusion.10
  129.6 0.2 select_reduce_fusion
  129.8 66.9 %all-gather.1 = f32[32,1,256]{2,1,0:T(1,128)S(1)} all-gather(f32[1,1,256]{2,1,0:T(1,128)S(1)} %bitcast.20), channel_id=2, replica_groups=mesh['grp'=16,'fsdp'=2] {'grp','fsdp'}, dimensions={0}, use_global_device_ids=true | all-gather | bytes 33792 | tf_op jit(solution)/shard_map/all_gather | solution.py:42
  196.7 0.1 reduce_sum.67
  196.8 0.6 fusion.23
  198.0 0.6 multiply_reduce_fusion
  199.3 0.0 copy-start.5
  199.4 6.4 %convolution_multiply_fusion = f32[1792,1024]{1,0:T(8,128)} fusion(bf16[1792,512]{1,0:T(8,128)(2,1)} %param.12, f32[256]{0:T(256)S(1)} %subtract_divide_fusion, bf16[256,1024]{1,0:T(8,128)(2,1)S(1)} %gather_fusion.1, pred[256]{0:T(512)(128)(4,1)S(1)} %get-tuple-element.3, s32[256]{0:T(256)S(1)} %bitcast.15), kind=kOutput, calls=%fused_computation.8 | convolution fusion | flops 1412562944 | bytes 9701632 | tf_op jit(solution)/shard_map/dot_general | solution.py:51
  205.8 0.0 copy-done.5
  (13 shorter events, 0.1 us)
Async XLA Ops:
  7.2 65.8 %copy-start = (bf16[512,1024]{1,0:T(8,128)(2,1)S(1)}, bf16[512,1024]{1,0:T(8,128)(2,1)}, u32[]{:S(2)}) copy-start(bf16[512,1024]{1,0:T(8,128)(2,1)} %param.13) | copy-start | bytes 3145732
  7.2 119.3 %reduce-scatter.2.cloned.1.call-start = ((), (), s32[]{:S(2)}) async-start(), calls=%async_computation.2 | async-start | bytes 7077888 | tf_op jit(solution)/shard_map/reduce_scatter | solution.py:17
  51.3 4.8 %copy-start.1 = (bf16[1792,512]{1,0:T(8,128)(2,1)S(1)}, bf16[1792,512]{1,0:T(8,128)(2,1)}, u32[]{:S(2)}) copy-start(bf16[1792,512]{1,0:T(8,128)(2,1)} %param.12) | copy-start | bytes 5505028
  65.7 0.7 copy-start.4
  65.7 1.5 copy-start.3
  73.0 2.5 %copy-start.2 = (bf16[384,1024]{1,0:T(8,128)(2,1)S(1)}, bf16[384,1024]{1,0:T(8,128)(2,1)}, u32[]{:S(2)}) copy-start(bf16[384,1024]{1,0:T(8,128)(2,1)} %param.10) | copy-start | bytes 2359300
  199.3 6.4 %copy-start.5 = (f32[256]{0:T(256)}, f32[256]{0:T(256)S(1)}, u32[]{:S(2)}) copy-start(f32[256]{0:T(256)S(1)} %subtract_divide_fusion) | copy-start | bytes 3076
Sparse Core Ops, SparseCore 0:
  65.9 60.5 reduce-scatter.1
